TPU v7x, 32 devices: a whole 2x2x4 slice. The times are simulated.
32 devices in a mesh: row: 4 (over y, x), col: 8 (over z, core).
Axes of the slice: x: 2, y: 2, z: 4, core: 2. Of those that a mesh axis runs over, the one named last changes fastest.
Arguments:
- amplitudes: bfloat16 [800, 800, 768], P('row', 'col'), may hold values from -6 to 6
- integrals: bfloat16 [800, 800, 256], P('row', 'col'), may hold values from -0.375 to 0.375
- window_index: int32 [256], replicated, may hold values from 0 to 639999, as said below
Outputs:
- residual: bfloat16 [800, 800, 768], P('row', 'col')
- pair_energy: float32 [768], replicated
Inputs may be any that keep to these rules, and one draw needn't show every extreme that they name: `window_index`: the window pairs are distinct; pair k lies in the block of a rows and b columns owned by device number k // 8 in row-major order of the (a, b) device grid, 8 pairs for each block.
All inputs are finite; a program needn't handle non-finite values.
Results may differ from a plain program's by a relative error of at most 0.001.
Values may be sent and summed in bfloat16 or wider, within the bound.
A program may use at most 256 MiB of HBM per device.

v0:
```python
import jax
import jax.numpy as jnp
from jax import lax
from jax.sharding import PartitionSpec as P


def shards(amplitudes, integrals, window_index):
    block_rows, block_cols, pairs = amplitudes.shape
    window = integrals.shape[2]
    ncols = lax.axis_size("col")
    nrows = lax.axis_size("row")
    per_device = window // (nrows * ncols)
    row_rank = lax.axis_index("row")
    col_rank = lax.axis_index("col")
    linear_rank = row_rank * ncols + col_rank
    owned_index = lax.dynamic_slice_in_dim(window_index, linear_rank * per_device, per_device)
    virtuals = block_rows * nrows
    row_offset = owned_index // virtuals - row_rank * block_rows
    col_offset = owned_index % virtuals - col_rank * block_cols
    owned = amplitudes[row_offset, col_offset]
    in_row = lax.all_gather(owned, "col", axis=0, tiled=True)
    columns = lax.all_gather(in_row, "row", axis=0, tiled=True)
    full = jnp.einsum("abk,kp->abp", integrals, columns, preferred_element_type=jnp.float32)
    partial_value = jnp.sum(amplitudes.astype(jnp.float32) * full, axis=(0, 1))
    pair_energy = lax.psum(partial_value, ("row", "col")) / virtuals
    residual = full.astype(jnp.bfloat16)
    return (residual, pair_energy)


def solution(mesh):
    return jax.shard_map(
        shards,
        mesh=mesh,
        in_specs=(P("row", "col", None), P("row", "col", None), P()),
        out_specs=(P("row", "col", None), P()),
        check_vma=False,
    )
```

profile of v0, /device:TPU:0, one launch (start us, length us, event | category | flops | bytes accessed | tf_op | source)
XLA Modules:
  0.0 172.8 jit_solution(1093921430304254708)
XLA Ops:
  0.6 0.8 fusion.7
  1.4 1.4 gather_fusion
  2.8 15.6 %all_gather.6 = bf16[64,768]{1,0:T(8,128)(2,1)S(1)} all-gather(bf16[8,768]{1,0:T(8,128)(2,1)S(1)} %gather_fusion), channel_id=1, replica_groups=mesh['row'=4,'col'=8] {'col'}, dimensions={0}, use_global_device_ids=true | all-gather | bytes 110592 | tf_op jit(solution)/shard_map/all_gather | solution.py:21
  18.4 9.5 %all_gather.7 = bf16[256,768]{1,0:T(8,128)(2,1)S(1)} all-gather(bf16[64,768]{1,0:T(8,128)(2,1)S(1)} %all_gather.6), channel_id=1, replica_groups=mesh['row'=4,'col'=8] {'row'}, dimensions={0}, use_global_device_ids=true | all-gather | bytes 491520 | tf_op jit(solution)/shard_map/all_gather | solution.py:22
  27.9 44.0 %bitcast_convert_fusion = (bf16[200,100,768]{2,1,0:T(8,128)(2,1)}, f32[768,200,100]{0,2,1:T(8,128)}) fusion(bf16[200,100,256]{2,0,1:T(8,128)(2,1)} %param.4, bf16[256,768]{1,0:T(8,128)(2,1)S(1)} %all_gather.7), kind=kOutput, calls=%fused_computation.2 | convolution fusion | flops 7879680000 | bytes 102793216 | tf_op jit(solution)/shard_map/abk,kp->abp/dot_general | solution.py:23
  71.9 22.0 %copy.7 = bf16[200,100,768]{2,0,1:T(8,128)(2,1)} copy(bf16[200,100,768]{2,1,0:T(8,128)(2,1)} %get-tuple-element.4) | data formatting | bytes 61440000
  93.9 39.0 %fusion = f32[768]{0:T(1024)S(1)} fusion(f32[768,200,100]{0,2,1:T(8,128)} %get-tuple-element.5, bf16[200,100,768]{2,0,1:T(8,128)(2,1)} %param.3), kind=kLoop, calls=%fused_computation.3 | loop fusion | flops 46079232 | bytes 92163072 | tf_op jit(solution)/shard_map/reduce_sum | solution.py:24
  132.9 39.3 %psum.7 = f32[768]{0:T(1024)S(1)} all-reduce(f32[768]{0:T(1024)S(1)} %fusion), channel_id=1, replica_groups=mesh['row'=4,'col'=8] {'row','col'}, use_global_device_ids=true, to_apply=%region_1.2 | all-reduce | flops 768 | bytes 6144 | tf_op jit(solution)/shard_map/psum | solution.py:25
  172.2 0.6 broadcast_multiply_fusion
where the time goes:
time: 173 us
  blocking collectives  64.5 us (37%)
  matrix products  44 us (25%)
  other arithmetic  40.3 us (23%)
  local copies, waits for them, and re-layouts  23.3 us (13%)
    dot_general x1, matrix products, shards(): jnp.einsum('abk,kp->abp', integrals, columns, preferred_element_type=jnp....  44 us
    psum x1, blocking collectives, shards(): pair_energy = lax.psum(partial_value, ('row', 'col')) / virtuals  39.3 us
    reduce_sum x1, other arithmetic, shards(): partial_value = jnp.sum(amplitudes.astype(jnp.float32) * full, axis=(0, 1))  39 us
    unnamed x1, local copies, waits for them, and re-layouts  22 us
    all_gather x1, blocking collectives, shards(): in_row = lax.all_gather(owned, 'col', axis=0, tiled=True)  15.6 us
    all_gather x1, blocking collectives, shards(): columns = lax.all_gather(in_row, 'row', axis=0, tiled=True)  9.5 us

commit v1 on v0

--- a/solution.py
+++ b/solution.py
@@ -18,7 +18,12 @@
     row_offset = owned_index // virtuals - row_rank * block_rows
     col_offset = owned_index % virtuals - col_rank * block_cols
     owned = amplitudes[row_offset, col_offset]
-    in_row = lax.all_gather(owned, "col", axis=0, tiled=True)
+    ring = [owned]
+    for hop in range(7):
+        ring.append(lax.ppermute(ring[-1], "col", [(dev, (dev + 1) % 8) for dev in range(8)]))
+    in_row = jnp.roll(
+        jnp.concatenate(ring[::-1], axis=0), (lax.axis_index("col") + 1) * ring[0].shape[0], axis=0
+    )
     columns = lax.all_gather(in_row, "row", axis=0, tiled=True)
     full = jnp.einsum("abk,kp->abp", integrals, columns, preferred_element_type=jnp.float32)
     partial_value = jnp.sum(amplitudes.astype(jnp.float32) * full, axis=(0, 1))

time: 173 us -> 192 us (1.11)
  waiting for transfers between devices: 0 us -> 34.9 us
  blocking collectives: 64.5 us -> 46.9 us
    ppermute x0 -> x7, waiting for transfers between devices: none -> 34.9 us  [shards(): lax.ppermute(ring[-1], 'col', [(dev, (dev + 1) % 8) for dev in range(8)])]
    all_gather x1 -> x0, blocking collectives: 15.6 us -> none  [shards(): in_row = lax.all_gather(owned, 'col', axis=0, tiled=True)]
    psum x1, blocking collectives: 39.3 us -> 36.9 us  [shards(): pair_energy = lax.psum(partial_value, ('row', 'col')) / virtuals]
    unnamed x1 -> x16, local copies, waits for them, and re-layouts: 22 us -> 22 us
  transfers between devices with their start and end apart: 0 -> 7, of which waited for: 0 -> 7; matrix products, arithmetic and copies ran while one was open for 0% -> 0% of each run, Pallas kernels for 0% -> 0%
where the time goes in v1:
time: 192 us; the launch traced here: 191 us
  blocking collectives  46.9 us (24%)
  matrix products  44.1 us (23%)
  other arithmetic  40.3 us (21%)
  waiting for transfers between devices  34.9 us (18%)
  local copies, waits for them, and re-layouts  23.4 us (12%)
    dot_general x1, matrix products, shards(): jnp.einsum('abk,kp->abp', integrals, columns, preferred_element_type=jnp....  44.1 us
    reduce_sum x1, other arithmetic, shards(): partial_value = jnp.sum(amplitudes.astype(jnp.float32) * full, axis=(0, 1))  39 us
    psum x1, blocking collectives, shards(): pair_energy = lax.psum(partial_value, ('row', 'col')) / virtuals  36.9 us
    ppermute x7, waiting for transfers between devices, shards(): lax.ppermute(ring[-1], 'col', [(dev, (dev + 1) % 8) for dev in range(8)])  34.9 us
    unnamed x16, local copies, waits for them, and re-layouts  22 us
    all_gather x1, blocking collectives, shards(): columns = lax.all_gather(in_row, 'row', axis=0, tiled=True)  10 us
  transfers between devices with their start and end apart: 7, of which 7 were waited for; matrix products, arithmetic and copies ran while one was open for 0% of the time, Pallas kernels for 0%

profile of v1, /device:TPU:0, one launch (start us, length us, event | category | flops | bytes accessed | tf_op | source)
XLA Modules:
  0.0 190.9 jit_solution(15600632935285199421)
XLA Ops:
  0.6 0.8 fusion.7
  1.4 1.4 gather_fusion
  2.8 0.5 collective-permute-start
  3.3 5.4 %collective-permute-done = bf16[8,768]{1,0:T(8,128)(2,1)S(1)} collective-permute-done((bf16[8,768]{1,0:T(8,128)(2,1)S(1)}, bf16[8,768]{1,0:T(8,128)(2,1)S(1)}, u32[]{:S(2)}, u32[]{:S(2)}) %collective-permute-start) | collective-permute-done | bytes 12320 | tf_op jit(solution)/shard_map/ppermute | solution.py:23
  8.7 0.0 collective-permute-start.1
  8.7 4.9 %collective-permute-done.1 = bf16[8,768]{1,0:T(8,128)(2,1)S(1)} collective-permute-done((bf16[8,768]{1,0:T(8,128)(2,1)S(1)}, bf16[8,768]{1,0:T(8,128)(2,1)S(1)}, u32[]{:S(2)}, u32[]{:S(2)}) %collective-permute-start.1) | collective-permute-done | bytes 12320 | tf_op jit(solution)/shard_map/ppermute | solution.py:23
  13.7 0.0 collective-permute-start.2
  13.7 4.9 %collective-permute-done.2 = bf16[8,768]{1,0:T(8,128)(2,1)S(1)} collective-permute-done((bf16[8,768]{1,0:T(8,128)(2,1)S(1)}, bf16[8,768]{1,0:T(8,128)(2,1)S(1)}, u32[]{:S(2)}, u32[]{:S(2)}) %collective-permute-start.2) | collective-permute-done | bytes 12320 | tf_op jit(solution)/shard_map/ppermute | solution.py:23
  18.6 0.0 collective-permute-start.3
  18.6 4.9 %collective-permute-done.3 = bf16[8,768]{1,0:T(8,128)(2,1)S(1)} collective-permute-done((bf16[8,768]{1,0:T(8,128)(2,1)S(1)}, bf16[8,768]{1,0:T(8,128)(2,1)S(1)}, u32[]{:S(2)}, u32[]{:S(2)}) %collective-permute-start.3) | collective-permute-done | bytes 12320 | tf_op jit(solution)/shard_map/ppermute | solution.py:23
  23.5 0.0 collective-permute-start.4
  23.5 4.9 %collective-permute-done.4 = bf16[8,768]{1,0:T(8,128)(2,1)S(1)} collective-permute-done((bf16[8,768]{1,0:T(8,128)(2,1)S(1)}, bf16[8,768]{1,0:T(8,128)(2,1)S(1)}, u32[]{:S(2)}, u32[]{:S(2)}) %collective-permute-start.4) | collective-permute-done | bytes 12320 | tf_op jit(solution)/shard_map/ppermute | solution.py:23
  28.4 0.0 collective-permute-start.5
  28.4 4.9 %collective-permute-done.5 = bf16[8,768]{1,0:T(8,128)(2,1)S(1)} collective-permute-done((bf16[8,768]{1,0:T(8,128)(2,1)S(1)}, bf16[8,768]{1,0:T(8,128)(2,1)S(1)}, u32[]{:S(2)}, u32[]{:S(2)}) %collective-permute-start.5) | collective-permute-done | bytes 12320 | tf_op jit(solution)/shard_map/ppermute | solution.py:23
  33.3 0.0 collective-permute-start.6
  33.3 4.9 %collective-permute-done.6 = bf16[8,768]{1,0:T(8,128)(2,1)S(1)} collective-permute-done((bf16[8,768]{1,0:T(8,128)(2,1)S(1)}, bf16[8,768]{1,0:T(8,128)(2,1)S(1)}, u32[]{:S(2)}, u32[]{:S(2)}) %collective-permute-start.6) | collective-permute-done | bytes 12320 | tf_op jit(solution)/shard_map/ppermute | solution.py:23
  38.4 10.0 %all_gather.3 = bf16[256,768]{1,0:T(8,128)(2,1)S(1)} all-gather(bf16[64,768]{1,0:T(8,128)(2,1)S(1)} %constant_dynamic-slice_fusion), channel_id=1, replica_groups=mesh['row'=4,'col'=8] {'row'}, dimensions={0}, use_global_device_ids=true | all-gather | bytes 491520 | tf_op jit(solution)/shard_map/all_gather | solution.py:27
  48.4 44.1 %bitcast_convert_fusion = (bf16[200,100,768]{2,1,0:T(8,128)(2,1)}, f32[768,200,100]{0,2,1:T(8,128)}) fusion(bf16[200,100,256]{2,0,1:T(8,128)(2,1)} %param.4, bf16[256,768]{1,0:T(8,128)(2,1)S(1)} %all_gather.3), kind=kOutput, calls=%fused_computation.2 | convolution fusion | flops 7879680000 | bytes 102793216 | tf_op jit(solution)/shard_map/abk,kp->abp/dot_general | solution.py:28
  92.5 22.0 %copy.7 = bf16[200,100,768]{2,0,1:T(8,128)(2,1)} copy(bf16[200,100,768]{2,1,0:T(8,128)(2,1)} %get-tuple-element.4) | data formatting | bytes 61440000
  114.5 39.0 %fusion = f32[768]{0:T(1024)S(1)} fusion(f32[768,200,100]{0,2,1:T(8,128)} %get-tuple-element.5, bf16[200,100,768]{2,0,1:T(8,128)(2,1)} %param.3), kind=kLoop, calls=%fused_computation.3 | loop fusion | flops 46079232 | bytes 92163072 | tf_op jit(solution)/shard_map/reduce_sum | solution.py:29
  153.4 36.9 %psum.7 = f32[768]{0:T(1024)S(1)} all-reduce(f32[768]{0:T(1024)S(1)} %fusion), channel_id=1, replica_groups=mesh['row'=4,'col'=8] {'row','col'}, use_global_device_ids=true, to_apply=%region_1.2 | all-reduce | flops 768 | bytes 6144 | tf_op jit(solution)/shard_map/psum | solution.py:30
  190.3 0.6 broadcast_multiply_fusion
  (17 shorter events, 0.1 us)
Async XLA Ops:
  2.8 5.9 %collective-permute-start = (bf16[8,768]{1,0:T(8,128)(2,1)S(1)}, bf16[8,768]{1,0:T(8,128)(2,1)S(1)}, u32[]{:S(2)}, u32[]{:S(2)}) collective-permute-start(bf16[8,768]{1,0:T(8,128)(2,1)S(1)} %gather_fusion), channel_id=1, source_target_pairs={{0,1},{1,2},{2,3},{3,4},{4,5},{5,6},{6,7},{7,0},{8,9},{9,10},{10,1... | collective-permute-start | bytes 36872 | tf_op jit(solution)/shard_map/ppermute | solution.py:23
  8.7 4.9 %collective-permute-start.1 = (bf16[8,768]{1,0:T(8,128)(2,1)S(1)}, bf16[8,768]{1,0:T(8,128)(2,1)S(1)}, u32[]{:S(2)}, u32[]{:S(2)}) collective-permute-start(bf16[8,768]{1,0:T(8,128)(2,1)S(1)} %collective-permute-done), channel_id=1, source_target_pairs={{0,1},{1,2},{2,3},{3,4},{4,5},{5,6},{6,7},{7,0},{8,9},{9,10},{10,1... | collective-permute-start | bytes 36872 | tf_op jit(solution)/shard_map/ppermute | solution.py:23
  13.7 4.9 %collective-permute-start.2 = (bf16[8,768]{1,0:T(8,128)(2,1)S(1)}, bf16[8,768]{1,0:T(8,128)(2,1)S(1)}, u32[]{:S(2)}, u32[]{:S(2)}) collective-permute-start(bf16[8,768]{1,0:T(8,128)(2,1)S(1)} %collective-permute-done.1), channel_id=1, source_target_pairs={{0,1},{1,2},{2,3},{3,4},{4,5},{5,6},{6,7},{7,0},{8,9},{9,10},{10,1... | collective-permute-start | bytes 36872 | tf_op jit(solution)/shard_map/ppermute | solution.py:23
  18.6 4.9 %collective-permute-start.3 = (bf16[8,768]{1,0:T(8,128)(2,1)S(1)}, bf16[8,768]{1,0:T(8,128)(2,1)S(1)}, u32[]{:S(2)}, u32[]{:S(2)}) collective-permute-start(bf16[8,768]{1,0:T(8,128)(2,1)S(1)} %collective-permute-done.2), channel_id=1, source_target_pairs={{0,1},{1,2},{2,3},{3,4},{4,5},{5,6},{6,7},{7,0},{8,9},{9,10},{10,1... | collective-permute-start | bytes 36872 | tf_op jit(solution)/shard_map/ppermute | solution.py:23
  23.5 4.9 %collective-permute-start.4 = (bf16[8,768]{1,0:T(8,128)(2,1)S(1)}, bf16[8,768]{1,0:T(8,128)(2,1)S(1)}, u32[]{:S(2)}, u32[]{:S(2)}) collective-permute-start(bf16[8,768]{1,0:T(8,128)(2,1)S(1)} %collective-permute-done.3), channel_id=1, source_target_pairs={{0,1},{1,2},{2,3},{3,4},{4,5},{5,6},{6,7},{7,0},{8,9},{9,10},{10,1... | collective-permute-start | bytes 36872 | tf_op jit(solution)/shard_map/ppermute | solution.py:23
  28.4 4.9 %collective-permute-start.5 = (bf16[8,768]{1,0:T(8,128)(2,1)S(1)}, bf16[8,768]{1,0:T(8,128)(2,1)S(1)}, u32[]{:S(2)}, u32[]{:S(2)}) collective-permute-start(bf16[8,768]{1,0:T(8,128)(2,1)S(1)} %collective-permute-done.4), channel_id=1, source_target_pairs={{0,1},{1,2},{2,3},{3,4},{4,5},{5,6},{6,7},{7,0},{8,9},{9,10},{10,1... | collective-permute-start | bytes 36872 | tf_op jit(solution)/shard_map/ppermute | solution.py:23
  33.3 4.9 %collective-permute-start.6 = (bf16[8,768]{1,0:T(8,128)(2,1)S(1)}, bf16[8,768]{1,0:T(8,128)(2,1)S(1)}, u32[]{:S(2)}, u32[]{:S(2)}) collective-permute-start(bf16[8,768]{1,0:T(8,128)(2,1)S(1)} %collective-permute-done.5), channel_id=1, source_target_pairs={{0,1},{1,2},{2,3},{3,4},{4,5},{5,6},{6,7},{7,0},{8,9},{9,10},{10,1... | collective-permute-start | bytes 36872 | tf_op jit(solution)/shard_map/ppermute | solution.py:23
